TPU v7x, 32 devices: a whole 2x2x4 slice. The times are simulated.
32 devices in a mesh: groups: 2 (over y), fft: 4 (over z), band: 2 (over x), sub: 2 (over core).
Axes of the slice: x: 2, y: 2, z: 4, core: 2. Of those that a mesh axis runs over, the one named last changes fastest.
Arguments:
- coefficients: bfloat16 [8, 2, 128, 1024], P(('groups', 'band', 'sub'), None, None, 'fft'), parts along dimension 0, may hold values from -6 to 6
- potential: float32 [384, 192, 192], P(('groups', 'fft')), parts along dimension 0, may hold values from -15 to 15
- stick_map: int32 [3, 2048], P(None, ('groups', 'fft')), parts along dimension 1, may hold values from 0 to 191, as said below
- plane_order: int32 [384], P('groups'), parts along dimension 0, may hold values from 0 to 191, each once
Outputs:
- applied: float32 [8, 2, 128, 1024], P(('groups', 'band', 'sub'), None, None, 'fft'), parts along dimension 0
There are 2 independent parts, one for each index of `groups`. A program takes and returns all parts, laid end to end along the dimension named above; each array names one. Nothing has to cross between parts.
Inputs may be any that keep to these rules, and one draw needn't show every extreme that they name: Column s is one stick slot: stick_map[0, s] and stick_map[1, s] are its grid indices x and y, stick_map[2, s] its length, an odd number up to 127, or 0 for an empty slot. A stick of length L holds the frequencies -(L - 1)/2 to (L - 1)/2 at entries 128/2 + f. The number of live slots differs between indices of fft; some index has all 256 slots live, and 512 slots are live in all. Live sticks name distinct columns, whose frequencies (indices taken modulo 192 into -96 to 95) lie in -48 to 47 along x and along y; an empty slot may name any column. `plane_order`: each plane number appears once.
All inputs are finite; a program needn't handle non-finite values.
Results may differ from a plain program's by a relative error of at most 0.0084.
Values may be sent and summed in bfloat16 or wider, within the bound.
No kernel may reach another device: no remote copies, remote signals or barrier semaphores. Data moves between devices by JAX's collectives and lax.ppermute only.
A program may use at most 128 MiB of HBM per device.

v0:
```python
import math
import jax
import jax.numpy as jnp
from jax import lax
from jax.sharding import PartitionSpec as P


def phase_tables(left_ids, right_ids, modulus):
    turn_index = left_ids[:, None] * right_ids[None, :] % modulus
    angles = turn_index.astype(jnp.float32) * (2.0 * math.pi / modulus)
    return (jnp.cos(angles).astype(jnp.bfloat16), jnp.sin(angles).astype(jnp.bfloat16))


def row_numbers(grid_side):
    compact = jnp.arange(grid_side // 2, dtype=jnp.int32)
    return jnp.where(compact < grid_side // 4, compact, compact + grid_side // 2)


def compact_rows(grid_ids, grid_side):
    rows = jnp.where(grid_ids < grid_side // 4, grid_ids, grid_ids - grid_side // 2)
    return jnp.clip(rows, 0, grid_side // 2 - 1)


def one_hot_rows(grid_ids, grid_side):
    rows = compact_rows(grid_ids, grid_side)
    slots = jnp.arange(grid_side // 2, dtype=jnp.int32)
    return (rows[:, None] == slots[None, :]).astype(jnp.bfloat16)


def plane_work(received, x_onehot, y_onehot, sources, depth_count, grid_side, potential_rows):
    planes = received.shape[0]
    half_side = grid_side // 2
    slot_count = x_onehot.shape[0] // sources

    def place_one(row):
        values = row.reshape(sources, depth_count, 2, slot_count).transpose(1, 2, 0, 3)
        values = values.reshape(depth_count, 2, sources * slot_count)
        weighted = values[..., None] * y_onehot[None, None]
        return jnp.einsum(
            "sx,dcsy->dxcy", x_onehot, weighted, preferred_element_type=jnp.float32
        ).astype(jnp.bfloat16)

    spread = lax.map(place_one, received)
    axis_ids = jnp.arange(grid_side, dtype=jnp.int32)
    live_ids = row_numbers(grid_side)
    cos_w, sin_w = phase_tables(live_ids, axis_ids, grid_side)
    forward_y = jnp.concatenate(
        [jnp.concatenate([cos_w, sin_w], 1), jnp.concatenate([-sin_w, cos_w], 1)], 0
    )
    inverse_y = jnp.concatenate(
        [jnp.concatenate([cos_w.T, -sin_w.T], 1), jnp.concatenate([sin_w.T, cos_w.T], 1)], 0
    )
    cos_x = cos_w.T
    sin_x = sin_w.T
    forward_x = jnp.concatenate([cos_x, sin_x], 0)
    inverse_x = jnp.concatenate([cos_w, sin_w], 0)
    half_y = jnp.dot(
        spread.reshape(-1, 2 * half_side), forward_y, preferred_element_type=jnp.float32
    )
    half_y = half_y.astype(jnp.bfloat16).reshape(planes, depth_count, half_side, 2 * grid_side)
    mixed_x = jnp.einsum("ux,pbxw->pbuw", forward_x, half_y, preferred_element_type=jnp.float32)
    cos_part = mixed_x[:, :, :grid_side]
    sin_part = mixed_x[:, :, grid_side:]
    pot_field = potential_rows[:, None, :, :]
    real_part = (cos_part[..., :grid_side] - sin_part[..., grid_side:]) * pot_field
    imag_part = (cos_part[..., grid_side:] + sin_part[..., :grid_side]) * pot_field
    product = jnp.concatenate([real_part, imag_part], 3).astype(jnp.bfloat16)
    mixed_x = jnp.einsum("ux,pbxw->pbuw", inverse_x, product, preferred_element_type=jnp.float32)
    cos_part = mixed_x[:, :, :half_side]
    sin_part = mixed_x[:, :, half_side:]
    back_x = jnp.concatenate(
        [
            cos_part[..., :grid_side] + sin_part[..., grid_side:],
            cos_part[..., grid_side:] - sin_part[..., :grid_side],
        ],
        3,
    ).astype(jnp.bfloat16)
    back_y = jnp.dot(
        back_x.reshape(-1, 2 * grid_side), inverse_y, preferred_element_type=jnp.float32
    ).astype(jnp.bfloat16)
    back_y = back_y.reshape(planes, depth_count, half_side, 2, half_side)

    def pick_one(grid):
        picked = jnp.einsum("sx,dxcy->dcsy", x_onehot, grid, preferred_element_type=jnp.float32)
        values = jnp.sum(picked * y_onehot[None, None], axis=3)
        values = values.reshape(depth_count, 2, sources, slot_count).transpose(2, 0, 1, 3)
        return values.reshape(-1).astype(jnp.bfloat16)

    return lax.map(pick_one, back_y)


def body(coefficients, potential, stick_map, plane_order):
    band_count = coefficients.shape[0]
    z_span = coefficients.shape[2]
    slot_count = coefficients.shape[3]
    grid_side = potential.shape[1]
    entries = jnp.arange(z_span, dtype=jnp.int32)
    freq_z = (entries - z_span // 2) % grid_side
    half_len = (stick_map[2] - 1) // 2
    keep_mask = jnp.abs(entries[:, None] - z_span // 2) <= half_len[None, :]
    masked = coefficients * keep_mask.astype(jnp.bfloat16)
    cos_z, sin_z = phase_tables(plane_order, freq_z, grid_side)
    forward_z = jnp.stack(
        [jnp.concatenate([cos_z, -sin_z], 1), jnp.concatenate([sin_z, cos_z], 1)], 1
    )
    sticks = jnp.einsum(
        "zck,bks->zbcs",
        forward_z,
        masked.reshape(band_count, 2 * z_span, slot_count),
        preferred_element_type=jnp.float32,
    )
    sticks = sticks.astype(jnp.bfloat16).reshape(grid_side, band_count * 2 * slot_count)
    columns = lax.all_gather(stick_map, "fft", axis=1, tiled=True)
    sources = lax.axis_size("fft")
    x_onehot = one_hot_rows(columns[0], grid_side)
    y_onehot = one_hot_rows(columns[1], grid_side)
    copies = lax.axis_size("sub")
    plane_share = potential.shape[0] // copies
    potential_rows = lax.dynamic_slice_in_dim(
        potential, lax.axis_index("sub") * plane_share, plane_share, 0
    )
    received = lax.all_to_all(sticks, ("fft", "sub"), split_axis=0, concat_axis=1, tiled=True)
    gathered = plane_work(
        received, x_onehot, y_onehot, sources, copies * band_count, grid_side, potential_rows
    )
    returned = lax.all_to_all(gathered, ("fft", "sub"), split_axis=1, concat_axis=0, tiled=True)
    inverse_z = jnp.stack([jnp.stack([cos_z, sin_z], 1), jnp.stack([-sin_z, cos_z], 1)], 1)
    totals = jnp.einsum(
        "rcdk,rbds->bcks",
        inverse_z,
        returned.reshape(grid_side, band_count, 2, slot_count),
        preferred_element_type=jnp.float32,
    )
    return totals * (keep_mask.astype(jnp.float32) * (1.0 / grid_side**3))


def solution(mesh):
    placed = (
        P(("groups", "band", "sub"), None, None, "fft"),
        P(("groups", "fft"), None, None),
        P(None, ("groups", "fft")),
        P("groups"),
    )
    return jax.shard_map(
        body,
        mesh=mesh,
        in_specs=placed,
        out_specs=P(("groups", "band", "sub"), None, None, "fft"),
        check_vma=False,
    )
```

profile of v0, /device:TPU:0, one launch (start us, length us, event | category | flops | bytes accessed | tf_op | source)
XLA Modules:
  0.0 154.8 jit_solution(12331591917178488166)
XLA Ops:
  0.0 1.2 sine_convert_fusion.3
  1.2 1.1 fusion.86
  2.3 0.7 and_select_fusion
  3.3 0.9 broadcast_multiply_fusion
  4.6 0.8 all_to_all.26
  5.4 6.4 %all-to-all-start = ((bf16[8,24,512]{2,1,0:T(8,128)(2,1)}), bf16[8,24,512]{2,1,0:T(8,128)(2,1)S(1)}, u32[]{:S(2)}, u32[]{:S(2)}) async-start(bf16[8,24,512]{2,1,0:T(8,128)(2,1)} %all_to_all.26), calls=%async_computation | async-start | bytes 393216 | tf_op jit(solution)/shard_map/all_to_all | solution.py:122
  11.8 15.4 %all_gather.3 = s32[3,1024]{1,0:T(4,128)S(1)} all-gather(s32[3,256]{1,0:T(4,128)} %param.10), channel_id=1, replica_groups=mesh['groups'=2,'fft'=4,'band'=2,'sub'=2] {'fft'}, dimensions={1}, use_global_device_ids=true | all-gather | bytes 15360 | tf_op jit(solution)/shard_map/all_gather | solution.py:113
  29.2 1.2 sine_convert_fusion
  30.3 1.1 fusion.87
  31.5 4.9 %constant_dynamic-slice_fusion.1 = f32[24,192,192]{2,1,0:T(8,128)} fusion(f32[48,192,192]{2,1,0:T(8,128)} %param.9, s32[]{:T(128)S(6)} %select_n.131), kind=kLoop, calls=%fused_computation.140 | loop fusion | bytes 7077892 | tf_op jit(solution)/shard_map/dynamic_slice | solution.py:119
  36.4 30.9 %while.22 = (s32[]{:T(128)}, bf16[24,2,96,2,96]{2,1,0,4,3:T(2,128)(2,1)}, bf16[24,4096]{1,0:T(8,128)(2,1)S(1)}, s32[1024]{0:T(1024)S(1)}, s32[1024]{0:T(1024)S(1)}, /*index=5*/s32[]{:T(128)}) while((s32[]{:T(128)}, bf16[24,2,96,2,96]{2,1,0,4,3:T(2,128)(2,1)}, bf16[24,4096]{1,0:T(8,128)(2,1)S(1)}, s32[1024]{0:T(1024)S(1)}, ...), condition=%wide.region_1.2_spmd.clone, body=%wide.region_0.1_spmd.clone.sunk | while | flops 76320768 | bytes 705097 | solution.py:43
  37.1 0.8 copy_dynamic-update-slice_fusion.2
  38.4 0.8 copy_dynamic-update-slice_fusion.2
  39.7 0.8 copy_dynamic-update-slice_fusion.2
  41.0 0.8 copy_dynamic-update-slice_fusion.2
  42.3 0.8 copy_dynamic-update-slice_fusion.2
  43.6 0.8 copy_dynamic-update-slice_fusion.2
  44.8 0.8 copy_dynamic-update-slice_fusion.2
  46.1 0.8 copy_dynamic-update-slice_fusion.2
  47.4 0.8 copy_dynamic-update-slice_fusion.2
  48.6 0.8 copy_dynamic-update-slice_fusion.2
  49.9 0.8 copy_dynamic-update-slice_fusion.2
  51.2 0.7 copy_dynamic-update-slice_fusion.2
  52.5 0.8 copy_dynamic-update-slice_fusion.2
  53.8 0.8 copy_dynamic-update-slice_fusion.2
  55.1 0.8 copy_dynamic-update-slice_fusion.2
  56.3 0.8 copy_dynamic-update-slice_fusion.2
  57.6 0.8 copy_dynamic-update-slice_fusion.2
  58.9 0.8 copy_dynamic-update-slice_fusion.2
  60.2 0.8 copy_dynamic-update-slice_fusion.2
  61.5 0.8 copy_dynamic-update-slice_fusion.2
  62.7 0.8 copy_dynamic-update-slice_fusion.2
  64.0 0.8 copy_dynamic-update-slice_fusion.2
  65.3 0.8 copy_dynamic-update-slice_fusion.2
  66.6 0.8 copy_dynamic-update-slice_fusion.2
  67.4 7.0 %reshape.324 = bf16[4608,192]{0,1:T(8,128)(2,1)S(1)} reshape(bf16[24,2,96,2,96]{2,1,0,4,3:T(2,128)(2,1)} %get-tuple-element.59) | data formatting | bytes 3538944 | tf_op jit(solution)/shard_map/reshape | solution.py:58
  74.4 1.5 convolution_convert_fusion.1
  75.9 11.5 %convolution_bitcast_fusion = f32[24,2,384,384]{3,2,1,0:T(8,128)} fusion(bf16[24,2,96,384]{3,2,1,0:T(8,128)(2,1)S(1)} %bitcast.104, bf16[192,96]{0,1:T(8,128)(2,1)S(1)} %get-tuple-element.141, bf16[192,96]{0,1:T(8,128)(2,1)S(1)} %get-tuple-element.140), kind=kOutput, calls=%fused_computation.28 | convolution fusion | flops 1359101952 | bytes 31924224 | tf_op jit(solution)/shard_map/ux,pbxw->pbuw/dot_general | solution.py:61
  87.3 16.3 %fusion.27 = (bf16[24,2,192,192]{3,2,1,0:T(8,128)(2,1)S(1)}, bf16[24,2,192,192]{3,2,1,0:T(8,128)(2,1)}) fusion(f32[24,2,384,384]{3,2,1,0:T(8,128)} %convolution_bitcast_fusion, f32[24,192,192]{2,1,0:T(8,128)S(1)} %bitcast.106), kind=kLoop, calls=%fused_computation.34 | loop fusion | flops 10616832 | bytes 38928384 | tf_op jit(solution)/shard_map/convert.4
  103.6 4.9 %convolution_bitcast_fusion.1 = f32[24,2,192,384]{3,2,1,0:T(8,128)S(1)} fusion(bf16[24,2,192,192]{3,2,1,0:T(8,128)(2,1)} %get-tuple-element.127, bf16[24,2,192,192]{3,2,1,0:T(8,128)(2,1)S(1)} %get-tuple-element.126, bf16[96,192]{1,0:T(8,128)(2,1)S(1)} %get-tuple-element.142, bf16[96,192]{1,0:T(8,128)(2,1)S(1)} %get-tuple-element.143), kind=kOutput, calls=%fused_computation.35 | convolution fusion | flops 1373257728 | bytes 21307392 | tf_op jit(solution)/shard_map/ux,pbxw->pbuw/dot_general | solution.py:68
  108.5 3.1 %fusion.32 = (bf16[24,2,96,192]{3,2,1,0:T(8,128)(2,1)S(1)}, bf16[24,2,96,192]{3,2,1,0:T(8,128)(2,1)S(1)}) fusion(f32[24,2,192,384]{3,2,1,0:T(8,128)S(1)} %convolution_bitcast_fusion.1), kind=kLoop, calls=%fused_computation.44 | loop fusion | flops 3538944 | bytes 17694720 | tf_op jit(solution)/shard_map/convert.3
  111.5 2.8 %convolution_convert_fusion.2 = bf16[4608,192]{0,1:T(8,128)(2,1)} fusion(bf16[4608,192]{1,0:T(8,128)(2,1)S(1)} %bitcast.108, bf16[4608,192]{1,0:T(8,128)(2,1)S(1)} %bitcast.107, bf16[192,96]{0,1:T(8,128)(2,1)S(1)} %get-tuple-element.140, bf16[192,96]{0,1:T(8,128)(2,1)S(1)} %get-tuple-element.141, bf16[192,96]{0,1:T(8,128)(2,1)S(1)} %fusion.85), kind=kOutput, calls=%fused_computation.40 | convolution fusion | flops 688029696 | bytes 5419008 | tf_op jit(solution)/shard_map/dot_general | solution.py:78
  114.3 7.7 %reshape.326 = bf16[24,2,96,2,96]{2,1,0,4,3:T(2,128)(2,1)S(1)} reshape(bf16[4608,192]{0,1:T(8,128)(2,1)} %convolution_convert_fusion.2) | data formatting | bytes 3538944 | tf_op jit(solution)/shard_map/reshape | solution.py:81
  122.0 19.3 %while.23 = (s32[]{:T(128)}, bf16[24,4096]{1,0:T(8,128)(2,1)S(1)}, bf16[24,2,96,2,96]{2,1,0,4,3:T(2,128)(2,1)S(1)}, s32[1024]{0:T(1024)S(1)}, s32[1024]{0:T(1024)S(1)}, /*index=5*/s32[]{:T(128)}, s32[]{:T(128)}) while((s32[]{:T(128)}, bf16[24,4096]{1,0:T(8,128)(2,1)S(1)}, bf16[24,2,96,2,96]{2,1,0,4,3:T(2,128)(2,1)S(1)}, ...), condition=%wide.region_4.5_spmd.clone, body=%wide.region_2.4_spmd.clone.sunk | while | flops 76771328 | bytes 1089621 | solution.py:89
  141.3 0.7 copy.44
  142.0 3.4 %all-to-all-start.1 = ((bf16[24,8,512]{2,0,1:T(8,128)(2,1)}), bf16[24,8,512]{2,0,1:T(8,128)(2,1)S(1)}, u32[]{:S(2)}, u32[]{:S(2)}) async-start(bf16[24,8,512]{2,0,1:T(8,128)(2,1)} %bitcast.87), calls=%async_computation.1 | async-start | bytes 393216 | tf_op jit(solution)/shard_map/all_to_all | solution.py:126
  145.5 8.1 %all-to-all-done.1 = bf16[24,8,512]{2,0,1:T(8,128)(2,1)S(1)} async-done(((bf16[24,8,512]{2,0,1:T(8,128)(2,1)}), bf16[24,8,512]{2,0,1:T(8,128)(2,1)S(1)}, u32[]{:S(2)}, u32[]{:S(2)}) %all-to-all-start.1) | async-done | bytes 196640 | tf_op jit(solution)/shard_map/all_to_all | solution.py:126
  153.9 0.8 copy.24
  (315 shorter events, 32.7 us)
Async XLA Ops:
  5.4 31.0 %all-to-all-start = ((bf16[8,24,512]{2,1,0:T(8,128)(2,1)}), bf16[8,24,512]{2,1,0:T(8,128)(2,1)S(1)}, u32[]{:S(2)}, u32[]{:S(2)}) async-start(bf16[8,24,512]{2,1,0:T(8,128)(2,1)} %all_to_all.26), calls=%async_computation | async-start | bytes 393216 | tf_op jit(solution)/shard_map/all_to_all | solution.py:122
  74.3 13.0 %slice-start = ((s8[4718592]{0:T(1024)(128)(4,1)}), s8[4194304]{0:T(1024)(128)(4,1)S(1)}, s32[]{:S(2)}) async-start(s8[4718592]{0:T(1024)(128)(4,1)} %bitcast.105), calls=%async_computation.2 | async-start | bytes 8388608
  75.9 11.5 %slice-start.1 = ((s8[4718592]{0:T(1024)(128)(4,1)}), s8[524288]{0:T(1024)(128)(4,1)S(1)}, s32[]{:S(2)}) async-start(s8[4718592]{0:T(1024)(128)(4,1)} %bitcast.105), calls=%async_computation.3 | async-start | bytes 1048576
  142.0 11.6 %all-to-all-start.1 = ((bf16[24,8,512]{2,0,1:T(8,128)(2,1)}), bf16[24,8,512]{2,0,1:T(8,128)(2,1)S(1)}, u32[]{:S(2)}, u32[]{:S(2)}) async-start(bf16[24,8,512]{2,0,1:T(8,128)(2,1)} %bitcast.87), calls=%async_computation.1 | async-start | bytes 393216 | tf_op jit(solution)/shard_map/all_to_all | solution.py:126
where the time goes:
time: 155 us
  local copies, waits for them, and re-layouts  51.1 us (33%)
  matrix products  38.7 us (25%)
  other arithmetic  29.4 us (19%)
  blocking collectives  15.4 us (10%)
  starting transfers between devices  9.75 us (6%)
  waiting for transfers between devices  8.1 us (5%)
  loops' own time  2.11 us (1%)
    another operation x2, other arithmetic  19.3 us
    dynamic_update_slice x24, local copies, waits for them, and re-layouts, plane_work(): spread = lax.map(place_one, received)  18.5 us
    all_gather x1, blocking collectives, body(): columns = lax.all_gather(stick_map, 'fft', axis=1, tiled=True)  15.4 us
    dot_general x1, matrix products, plane_work(): jnp.einsum('ux,pbxw->pbuw', forward_x, half_y, preferred_element_type=jnp...  11.5 us
    dot_general x24, matrix products, pick_one(): jnp.einsum('sx,dxcy->dcsy', x_onehot, grid, preferred_element_type=jnp.fl...  8.95 us
    dot_general x24, matrix products, place_one(): jnp.einsum('sx,dcsy->dxcy', x_onehot, weighted, preferred_element_type=jn...  8.66 us
    all_to_all x1, waiting for transfers between devices, body(): lax.all_to_all(gathered, ('fft', 'sub'), split_axis=1, concat_axis=0, til...  8.1 us
    reshape x1, local copies, waits for them, and re-layouts, plane_work(): back_y = back_y.reshape(planes, depth_count, half_side, 2, half_side)  7.68 us
  transfers between devices with their start and end apart: 2, of which 1 were waited for; matrix products, arithmetic and copies ran while one was open for 6% of the time, Pallas kernels for 0%

commit v1 on v0

--- a/solution.py
+++ b/solution.py
@@ -110,7 +110,12 @@
         preferred_element_type=jnp.float32,
     )
     sticks = sticks.astype(jnp.bfloat16).reshape(grid_side, band_count * 2 * slot_count)
-    columns = lax.all_gather(stick_map, "fft", axis=1, tiled=True)
+    ring = [stick_map]
+    for hop in range(3):
+        ring.append(lax.ppermute(ring[-1], "fft", [(dev, (dev + 1) % 4) for dev in range(4)]))
+    columns = jnp.roll(
+        jnp.concatenate(ring[::-1], axis=1), (lax.axis_index("fft") + 1) * ring[0].shape[1], axis=1
+    )
     sources = lax.axis_size("fft")
     x_onehot = one_hot_rows(columns[0], grid_side)
     y_onehot = one_hot_rows(columns[1], grid_side)

time: 155 us -> 150 us (0.968)
  blocking collectives: 15.4 us -> 0 us
  waiting for transfers between devices: 8.1 us -> 15.7 us
  starting transfers between devices: 9.75 us -> 12.6 us
    all_gather x1 -> x0, blocking collectives: 15.4 us -> none  [body(): columns = lax.all_gather(stick_map, 'fft', axis=1, tiled=True)]
    ppermute x0 -> x3, waiting for transfers between devices: none -> 7.6 us  [body(): lax.ppermute(ring[-1], 'fft', [(dev, (dev + 1) % 4) for dev in range(4)])]
    ppermute x0 -> x3, starting transfers between devices: none -> 5.35 us  [body(): lax.ppermute(ring[-1], 'fft', [(dev, (dev + 1) % 4) for dev in range(4)])]
    all_to_all x1, starting transfers between devices: 6.35 us -> 3.87 us  [body(): lax.all_to_all(sticks, ('fft', 'sub'), split_axis=0, concat_axis=1, tiled...]
  transfers between devices with their start and end apart: 2 -> 5, of which waited for: 1 -> 3; matrix products, arithmetic and copies ran while one was open for 6% -> 9% of each run, Pallas kernels for 0% -> 0%
where the time goes in v1:
time: 150 us; the launch traced here: 149 us
  local copies, waits for them, and re-layouts  51.3 us (34%)
  matrix products  38.7 us (26%)
  other arithmetic  28.8 us (19%)
  waiting for transfers between devices  15.7 us (10%)
  starting transfers between devices  12.6 us (8%)
  loops' own time  2.11 us (1%)
    another operation x2, other arithmetic  19.4 us
    dynamic_update_slice x24, local copies, waits for them, and re-layouts, plane_work(): spread = lax.map(place_one, received)  18.5 us
    dot_general x1, matrix products, plane_work(): jnp.einsum('ux,pbxw->pbuw', forward_x, half_y, preferred_element_type=jnp...  11.5 us
    dot_general x24, matrix products, pick_one(): jnp.einsum('sx,dxcy->dcsy', x_onehot, grid, preferred_element_type=jnp.fl...  8.95 us
    dot_general x24, matrix products, place_one(): jnp.einsum('sx,dcsy->dxcy', x_onehot, weighted, preferred_element_type=jn...  8.66 us
    all_to_all x1, waiting for transfers between devices, body(): lax.all_to_all(gathered, ('fft', 'sub'), split_axis=1, concat_axis=0, til...  8.1 us
    reshape x1, local copies, waits for them, and re-layouts, plane_work(): back_y = back_y.reshape(planes, depth_count, half_side, 2, half_side)  7.68 us
    ppermute x3, waiting for transfers between devices, body(): lax.ppermute(ring[-1], 'fft', [(dev, (dev + 1) % 4) for dev in range(4)])  7.6 us
  transfers between devices with their start and end apart: 5, of which 3 were waited for; matrix products, arithmetic and copies ran while one was open for 9% of the time, Pallas kernels for 0%

profile of v1, /device:TPU:0, one launch (start us, length us, event | category | flops | bytes accessed | tf_op | source)
XLA Modules:
  0.0 149.5 jit_solution(10158774263587530826)
XLA Ops:
  0.0 3.1 %collective-permute-start = (s32[3,256]{1,0:T(4,128)}, s32[3,256]{1,0:T(4,128)S(1)}, u32[]{:S(2)}, u32[]{:S(2)}) collective-permute-start(s32[3,256]{1,0:T(4,128)} %param.10), channel_id=1, source_target_pairs={{0,4},{4,8},{8,12},{12,0},{1,5},{5,9},{9,13},{13,1},{2,6},{6,10},{... | collective-permute-start | bytes 9224 | tf_op jit(solution)/shard_map/ppermute | solution.py:115
  3.1 1.2 sine_convert_fusion.3
  4.2 1.1 fusion.86
  6.3 0.9 broadcast_multiply_fusion
  7.7 0.8 all_to_all.26
  8.5 3.9 %all-to-all-start = ((bf16[8,24,512]{2,1,0:T(8,128)(2,1)}), bf16[8,24,512]{2,1,0:T(8,128)(2,1)S(1)}, u32[]{:S(2)}, u32[]{:S(2)}) async-start(bf16[8,24,512]{2,1,0:T(8,128)(2,1)} %all_to_all.26), calls=%async_computation | async-start | bytes 393216 | tf_op jit(solution)/shard_map/all_to_all | solution.py:127
  13.4 1.2 sine_convert_fusion
  14.6 4.9 %constant_dynamic-slice_fusion.1 = f32[24,192,192]{2,1,0:T(8,128)} fusion(f32[48,192,192]{2,1,0:T(8,128)} %param.9, s32[]{:T(128)S(6)} %select_n.145), kind=kLoop, calls=%fused_computation.148 | loop fusion | bytes 7077892 | tf_op jit(solution)/shard_map/dynamic_slice | solution.py:124
  20.0 2.1 %collective-permute-start.1 = (s32[3,256]{1,0:T(4,128)S(1)}, s32[3,256]{1,0:T(4,128)S(1)}, u32[]{:S(2)}, u32[]{:S(2)}) collective-permute-start(s32[3,256]{1,0:T(4,128)S(1)} %collective-permute-done), channel_id=1, source_target_pairs={{0,4},{4,8},{8,12},{12,0},{1,5},{5,9},{9,13},{13,1},{2,6},{6,10},{... | collective-permute-start | bytes 9224 | tf_op jit(solution)/shard_map/ppermute | solution.py:115
  22.5 2.9 %collective-permute-done.1 = s32[3,256]{1,0:T(4,128)S(1)} collective-permute-done((s32[3,256]{1,0:T(4,128)S(1)}, s32[3,256]{1,0:T(4,128)S(1)}, u32[]{:S(2)}, u32[]{:S(2)}) %collective-permute-start.1) | collective-permute-done | bytes 3104 | tf_op jit(solution)/shard_map/ppermute | solution.py:115
  26.1 4.7 %collective-permute-done.2 = s32[3,256]{1,0:T(4,128)S(1)} collective-permute-done((s32[3,256]{1,0:T(4,128)S(1)}, s32[3,256]{1,0:T(4,128)S(1)}, u32[]{:S(2)}, u32[]{:S(2)}) %collective-permute-start.2) | collective-permute-done | bytes 3104 | tf_op jit(solution)/shard_map/ppermute | solution.py:115
  31.0 31.0 %while.22 = (s32[]{:T(128)}, bf16[24,2,96,2,96]{2,1,0,4,3:T(2,128)(2,1)}, bf16[24,4096]{1,0:T(8,128)(2,1)S(1)}, s32[1024]{0:T(1024)S(1)}, s32[1024]{0:T(1024)S(1)}, /*index=5*/s32[]{:T(128)}) while((s32[]{:T(128)}, bf16[24,2,96,2,96]{2,1,0,4,3:T(2,128)(2,1)}, bf16[24,4096]{1,0:T(8,128)(2,1)S(1)}, s32[1024]{0:T(1024)S(1)}, ...), condition=%wide.region_1.2_spmd.clone, body=%wide.region_0.1_spmd.clone.sunk | while | flops 76320768 | bytes 705097 | solution.py:43
  31.7 0.8 copy_dynamic-update-slice_fusion.2
  33.0 0.8 copy_dynamic-update-slice_fusion.2
  34.3 0.8 copy_dynamic-update-slice_fusion.2
  35.6 0.8 copy_dynamic-update-slice_fusion.2
  36.9 0.8 copy_dynamic-update-slice_fusion.2
  38.1 0.8 copy_dynamic-update-slice_fusion.2
  39.4 0.8 copy_dynamic-update-slice_fusion.2
  40.7 0.8 copy_dynamic-update-slice_fusion.2
  42.0 0.8 copy_dynamic-update-slice_fusion.2
  43.3 0.8 copy_dynamic-update-slice_fusion.2
  44.6 0.8 copy_dynamic-update-slice_fusion.2
  45.8 0.8 copy_dynamic-update-slice_fusion.2
  47.1 0.8 copy_dynamic-update-slice_fusion.2
  48.4 0.8 copy_dynamic-update-slice_fusion.2
  49.7 0.8 copy_dynamic-update-slice_fusion.2
  50.9 0.8 copy_dynamic-update-slice_fusion.2
  52.2 0.8 copy_dynamic-update-slice_fusion.2
  53.5 0.8 copy_dynamic-update-slice_fusion.2
  54.8 0.8 copy_dynamic-update-slice_fusion.2
  56.1 0.8 copy_dynamic-update-slice_fusion.2
  57.3 0.8 copy_dynamic-update-slice_fusion.2
  58.6 0.8 copy_dynamic-update-slice_fusion.2
  59.9 0.8 copy_dynamic-update-slice_fusion.2
  61.2 0.8 copy_dynamic-update-slice_fusion.2
  62.0 7.0 %reshape.324 = bf16[4608,192]{0,1:T(8,128)(2,1)S(1)} reshape(bf16[24,2,96,2,96]{2,1,0,4,3:T(2,128)(2,1)} %get-tuple-element.59) | data formatting | bytes 3538944 | tf_op jit(solution)/shard_map/reshape | solution.py:58
  69.0 1.5 %convolution_convert_fusion.1 = bf16[4608,384]{1,0:T(8,128)(2,1)S(1)} fusion(bf16[4608,192]{0,1:T(8,128)(2,1)S(1)} %reshape.324, bf16[96,192]{1,0:T(8,128)(2,1)S(1)} %get-tuple-element.143, bf16[96,192]{1,0:T(8,128)(2,1)S(1)} %fusion.84, bf16[96,192]{1,0:T(8,128)(2,1)S(1)} %get-tuple-element.142), kind=kOutput, calls=%fused_computation.39 | convolution fusion | flops 681836544 | bytes 5419008 | tf_op jit(solution)/shard_map/dot_general | solution.py:57
  70.5 11.5 %convolution_bitcast_fusion = f32[24,2,384,384]{3,2,1,0:T(8,128)} fusion(bf16[24,2,96,384]{3,2,1,0:T(8,128)(2,1)S(1)} %bitcast.104, bf16[192,96]{0,1:T(8,128)(2,1)S(1)} %get-tuple-element.141, bf16[192,96]{0,1:T(8,128)(2,1)S(1)} %get-tuple-element.140), kind=kOutput, calls=%fused_computation.28 | convolution fusion | flops 1359101952 | bytes 31924224 | tf_op jit(solution)/shard_map/ux,pbxw->pbuw/dot_general | solution.py:61
  82.0 16.3 %fusion.27 = (bf16[24,2,192,192]{3,2,1,0:T(8,128)(2,1)S(1)}, bf16[24,2,192,192]{3,2,1,0:T(8,128)(2,1)}) fusion(f32[24,2,384,384]{3,2,1,0:T(8,128)} %convolution_bitcast_fusion, f32[24,192,192]{2,1,0:T(8,128)S(1)} %bitcast.106), kind=kLoop, calls=%fused_computation.34 | loop fusion | flops 10616832 | bytes 38928384 | tf_op jit(solution)/shard_map/convert.4
  98.3 4.9 %convolution_bitcast_fusion.1 = f32[24,2,192,384]{3,2,1,0:T(8,128)S(1)} fusion(bf16[24,2,192,192]{3,2,1,0:T(8,128)(2,1)} %get-tuple-element.127, bf16[24,2,192,192]{3,2,1,0:T(8,128)(2,1)S(1)} %get-tuple-element.126, bf16[96,192]{1,0:T(8,128)(2,1)S(1)} %get-tuple-element.142, bf16[96,192]{1,0:T(8,128)(2,1)S(1)} %get-tuple-element.143), kind=kOutput, calls=%fused_computation.35 | convolution fusion | flops 1373257728 | bytes 21307392 | tf_op jit(solution)/shard_map/ux,pbxw->pbuw/dot_general | solution.py:68
  103.1 3.1 %fusion.32 = (bf16[24,2,96,192]{3,2,1,0:T(8,128)(2,1)S(1)}, bf16[24,2,96,192]{3,2,1,0:T(8,128)(2,1)S(1)}) fusion(f32[24,2,192,384]{3,2,1,0:T(8,128)S(1)} %convolution_bitcast_fusion.1), kind=kLoop, calls=%fused_computation.44 | loop fusion | flops 3538944 | bytes 17694720 | tf_op jit(solution)/shard_map/convert.3
  106.2 2.8 %convolution_convert_fusion.2 = bf16[4608,192]{0,1:T(8,128)(2,1)} fusion(bf16[4608,192]{1,0:T(8,128)(2,1)S(1)} %bitcast.108, bf16[4608,192]{1,0:T(8,128)(2,1)S(1)} %bitcast.107, bf16[192,96]{0,1:T(8,128)(2,1)S(1)} %get-tuple-element.140, bf16[192,96]{0,1:T(8,128)(2,1)S(1)} %get-tuple-element.141, bf16[192,96]{0,1:T(8,128)(2,1)S(1)} %fusion.85), kind=kOutput, calls=%fused_computation.40 | convolution fusion | flops 688029696 | bytes 5419008 | tf_op jit(solution)/shard_map/dot_general | solution.py:78
  109.0 7.7 %reshape.326 = bf16[24,2,96,2,96]{2,1,0,4,3:T(2,128)(2,1)S(1)} reshape(bf16[4608,192]{0,1:T(8,128)(2,1)} %convolution_convert_fusion.2) | data formatting | bytes 3538944 | tf_op jit(solution)/shard_map/reshape | solution.py:81
  116.7 19.3 %while.23 = (s32[]{:T(128)}, bf16[24,4096]{1,0:T(8,128)(2,1)S(1)}, bf16[24,2,96,2,96]{2,1,0,4,3:T(2,128)(2,1)S(1)}, s32[1024]{0:T(1024)S(1)}, s32[1024]{0:T(1024)S(1)}, /*index=5*/s32[]{:T(128)}, s32[]{:T(128)}) while((s32[]{:T(128)}, bf16[24,4096]{1,0:T(8,128)(2,1)S(1)}, bf16[24,2,96,2,96]{2,1,0,4,3:T(2,128)(2,1)S(1)}, ...), condition=%wide.region_4.5_spmd.clone, body=%wide.region_2.4_spmd.clone.sunk | while | flops 76771328 | bytes 1089621 | solution.py:89
  136.7 3.4 %all-to-all-start.1 = ((bf16[24,8,512]{2,0,1:T(8,128)(2,1)}), bf16[24,8,512]{2,0,1:T(8,128)(2,1)S(1)}, u32[]{:S(2)}, u32[]{:S(2)}) async-start(bf16[24,8,512]{2,0,1:T(8,128)(2,1)} %bitcast.87), calls=%async_computation.1 | async-start | bytes 393216 | tf_op jit(solution)/shard_map/all_to_all | solution.py:131
  140.2 8.1 %all-to-all-done.1 = bf16[24,8,512]{2,0,1:T(8,128)(2,1)S(1)} async-done(((bf16[24,8,512]{2,0,1:T(8,128)(2,1)}), bf16[24,8,512]{2,0,1:T(8,128)(2,1)S(1)}, u32[]{:S(2)}, u32[]{:S(2)}) %all-to-all-start.1) | async-done | bytes 196640 | tf_op jit(solution)/shard_map/all_to_all | solution.py:131
  148.6 0.8 copy.24
  (332 shorter events, 34.9 us)
Async XLA Ops:
  0.0 19.9 %collective-permute-start = (s32[3,256]{1,0:T(4,128)}, s32[3,256]{1,0:T(4,128)S(1)}, u32[]{:S(2)}, u32[]{:S(2)}) collective-permute-start(s32[3,256]{1,0:T(4,128)} %param.10), channel_id=1, source_target_pairs={{0,4},{4,8},{8,12},{12,0},{1,5},{5,9},{9,13},{13,1},{2,6},{6,10},{... | collective-permute-start | bytes 9224 | tf_op jit(solution)/shard_map/ppermute | solution.py:115
  8.5 22.5 %all-to-all-start = ((bf16[8,24,512]{2,1,0:T(8,128)(2,1)}), bf16[8,24,512]{2,1,0:T(8,128)(2,1)S(1)}, u32[]{:S(2)}, u32[]{:S(2)}) async-start(bf16[8,24,512]{2,1,0:T(8,128)(2,1)} %all_to_all.26), calls=%async_computation | async-start | bytes 393216 | tf_op jit(solution)/shard_map/all_to_all | solution.py:127
  14.5 4.9 %copy-start.1 = (s32[192]{0:T(256)S(1)}, s32[192]{0:T(256)}, u32[]{:S(2)}) copy-start(s32[192]{0:T(256)} %param.11) | copy-start | bytes 2308
  14.6 16.3 %copy-start = (s32[3,256]{1,0:T(4,128)S(1)}, s32[3,256]{1,0:T(4,128)}, u32[]{:S(2)}) copy-start(s32[3,256]{1,0:T(4,128)} %param.10) | copy-start | bytes 9220
  20.0 5.5 %collective-permute-start.1 = (s32[3,256]{1,0:T(4,128)S(1)}, s32[3,256]{1,0:T(4,128)S(1)}, u32[]{:S(2)}, u32[]{:S(2)}) collective-permute-start(s32[3,256]{1,0:T(4,128)S(1)} %collective-permute-done), channel_id=1, source_target_pairs={{0,4},{4,8},{8,12},{12,0},{1,5},{5,9},{9,13},{13,1},{2,6},{6,10},{... | collective-permute-start | bytes 9224 | tf_op jit(solution)/shard_map/ppermute | solution.py:115
  25.4 5.4 %collective-permute-start.2 = (s32[3,256]{1,0:T(4,128)S(1)}, s32[3,256]{1,0:T(4,128)S(1)}, u32[]{:S(2)}, u32[]{:S(2)}) collective-permute-start(s32[3,256]{1,0:T(4,128)S(1)} %collective-permute-done.1), channel_id=1, source_target_pairs={{0,4},{4,8},{8,12},{12,0},{1,5},{5,9},{9,13},{13,1},{2,6},{6,10},{... | collective-permute-start | bytes 9224 | tf_op jit(solution)/shard_map/ppermute | solution.py:115
  69.0 13.0 %slice-start = ((s8[4718592]{0:T(1024)(128)(4,1)}), s8[4194304]{0:T(1024)(128)(4,1)S(1)}, s32[]{:S(2)}) async-start(s8[4718592]{0:T(1024)(128)(4,1)} %bitcast.105), calls=%async_computation.2 | async-start | bytes 8388608
  70.5 11.5 %slice-start.1 = ((s8[4718592]{0:T(1024)(128)(4,1)}), s8[524288]{0:T(1024)(128)(4,1)S(1)}, s32[]{:S(2)}) async-start(s8[4718592]{0:T(1024)(128)(4,1)} %bitcast.105), calls=%async_computation.3 | async-start | bytes 1048576
  136.7 11.6 %all-to-all-start.1 = ((bf16[24,8,512]{2,0,1:T(8,128)(2,1)}), bf16[24,8,512]{2,0,1:T(8,128)(2,1)S(1)}, u32[]{:S(2)}, u32[]{:S(2)}) async-start(bf16[24,8,512]{2,0,1:T(8,128)(2,1)} %bitcast.87), calls=%async_computation.1 | async-start | bytes 393216 | tf_op jit(solution)/shard_map/all_to_all | solution.py:131
